TPU v7x, 32 devices: a whole 2x2x4 slice. The times are simulated.
32 devices in a mesh: terms: 2 (over x), rows: 4 (over y, core), cols: 4 (over z).
Axes of the slice: x: 2, y: 2, z: 4, core: 2. Of those that a mesh axis runs over, the one named last changes fastest.
Arguments:
- wavefunction: bfloat16 [2, 1024, 1024], P(None, 'rows', 'cols'), may hold values from -6 to 6
- energy: float32 [2], replicated, may hold values from 1 to 4
- block_rows: int32 [2], replicated, may hold values from 512 to 1024
- block_cols: int32 [2], replicated, may hold values from 512 to 1024
- left_ops: bfloat16 [8, 1024, 1024], P('terms', 'rows'), may hold values from -0.1875 to 0.1875
- right_ops: bfloat16 [8, 1024, 1024], P('terms', 'cols'), may hold values from -0.1875 to 0.1875
- source: int32 [8], P('terms'), may hold values from 0 to 1
- target: int32 [8], P('terms'), may hold values from 0 to 1
Outputs:
- sigma: bfloat16 [2, 1024, 1024], P(None, 'rows', 'cols')
- residual: bfloat16 [2, 1024, 1024], P(None, 'rows', 'cols')
Inputs may be any that keep to these rules, and one draw needn't show every extreme that they name: source[t] is the sector whose block term t reads. target[t] is the sector to which term t adds. `block_rows`: entries of a sector block beyond its live left or right states are ignored.
All inputs are finite; a program needn't handle non-finite values.
Results may differ from a plain program's by a relative error of at most 0.0044.
The roundings to bfloat16 on the way count: a program that leaves them out, or rounds other values in their place, can miss the bound.
Values may be sent and summed in bfloat16 or wider, within the bound.
No kernel may reach another device: no remote copies, remote signals or barrier semaphores. Data moves between devices by JAX's collectives and lax.ppermute only.
A program may use at most 64 MiB of HBM per device.

v0:
```python
import jax
import jax.numpy as jnp
from jax import lax
from jax.sharding import PartitionSpec as P

EPSILON = 1e-06


def per_device(wavefunction, energy, block_rows, block_cols, left_ops, right_ops, source, target):
    sectors, tile_rows, tile_cols = wavefunction.shape
    term_count = left_ops.shape[0]
    row_ids = lax.axis_index("rows") * tile_rows + lax.iota(jnp.int32, tile_rows)
    col_ids = lax.axis_index("cols") * tile_cols + lax.iota(jnp.int32, tile_cols)
    inside = (row_ids[None, :, None] < block_rows[:, None, None]) & (
        col_ids[None, None, :] < block_cols[:, None, None]
    )
    live_psi = jnp.where(inside, wavefunction, jnp.zeros_like(wavefunction))
    sector_ids = lax.iota(jnp.int32, sectors)
    partial_value = jnp.zeros((sectors, tile_rows, tile_cols), jnp.float32)
    panels = lax.all_gather(live_psi, "rows", axis=1, tiled=True)
    product_list = []
    for term_index in range(term_count):
        col_panel = lax.dynamic_index_in_dim(panels, source[term_index], 0, keepdims=False)
        product_list.append(
            jnp.dot(left_ops[term_index], col_panel, preferred_element_type=jnp.float32).astype(
                jnp.bfloat16
            )
        )
    products = jnp.stack(product_list)
    additions = jnp.einsum(
        "txl,tml->txm",
        lax.all_gather(products, "cols", axis=2, tiled=True),
        right_ops,
        preferred_element_type=jnp.float32,
    )
    for term_index in range(term_count):
        hit = (sector_ids == target[term_index])[:, None, None]
        partial_value = partial_value + jnp.where(hit, additions[term_index][None], 0.0)
    live_f = live_psi.astype(jnp.float32)
    summed = lax.psum(partial_value, "terms")
    full_sigma = jnp.where(inside, summed + energy[:, None, None] * live_f, 0.0)
    numerator, denominator = lax.psum(
        (jnp.sum(live_f * full_sigma), jnp.sum(live_f * live_f)), ("rows", "cols")
    )
    rayleigh = numerator / (denominator + EPSILON)
    residual = full_sigma - rayleigh * live_f
    return (full_sigma.astype(jnp.bfloat16), residual.astype(jnp.bfloat16))


def solution(mesh):
    in_specs = (
        P(None, "rows", "cols"),
        P(),
        P(),
        P(),
        P("terms", "rows", None),
        P("terms", "cols", None),
        P("terms"),
        P("terms"),
    )
    out_specs = (P(None, "rows", "cols"), P(None, "rows", "cols"))
    return jax.shard_map(
        per_device, mesh=mesh, in_specs=in_specs, out_specs=out_specs, check_vma=False
    )
```

profile of v0, /device:TPU:0, one launch (start us, length us, event | category | flops | bytes accessed | tf_op | source)
XLA Modules:
  0.0 158.2 jit_solution(4470335550946866538)
XLA Ops:
  7.2 0.0 copy-start
  7.2 0.0 all-gather.3.cloned.1.call-start
  7.3 0.9 broadcast_compare_fusion
  8.1 1.8 %and_select_fusion.1 = bf16[2,256,256]{2,1,0:T(8,128)(2,1)} fusion(bf16[2,256,256]{2,1,0:T(8,128)(2,1)} %param.8, pred[2,256]{1,0:T(4,128)(4,1)S(1)} %get-tuple-element.20, pred[2,256]{1,0:T(4,128)(4,1)S(1)} %get-tuple-element.21), kind=kLoop, calls=%fused_computation.13 | loop fusion | flops 262144 | bytes 525312 | tf_op jit(solution)/shard_map/jit(_where)/select_n | solution.py:17
  9.9 0.0 all-gather.3.cloned.1.call-update
  10.0 0.0 all-gather.5.cloned.1.call-start
  10.0 1.5 fusion.31
  19.3 10.4 %all-gather.3.cloned.1.call-done = bf16[2,1024,256]{2,1,0:T(8,128)(2,1)} async-done(((bf16[2,256,256]{2,1,0:T(8,128)(2,1)}), bf16[2,1024,256]{2,1,0:T(8,128)(2,1)}) %all-gather.3.cloned.1.call-update) | async-done | bytes 1048592 | tf_op jit(solution)/shard_map/all_gather | solution.py:20
  29.6 0.0 copy-start.4
  29.6 0.0 copy-start.5
  29.6 1.7 %fusion = bf16[1,256,256]{1,2,0:T(8,128)(2,1)S(1)} fusion(bf16[4,256,1024]{2,1,0:T(8,128)(2,1)} %param.12, bf16[2,1024,256]{2,1,0:T(8,128)(2,1)} %all-gather.3.cloned.1.call-done, s32[]{:T(128)S(6)} %select_n.35), kind=kOutput, calls=%fused_computation.4 | convolution fusion | flops 134283264 | bytes 1179652 | tf_op jit(solution)/shard_map/dot_general | solution.py:25
  31.3 1.6 fusion.1
  32.9 0.0 copy-done.4
  32.9 0.0 copy-start.2
  32.9 1.4 fusion.2
  34.3 0.0 copy-done.5
  34.3 0.4 fusion.3
  34.7 0.9 pad_maximum_fusion
  35.6 0.0 all-gather.5.cloned.1.call-update
  35.6 0.0 all-reduce.3.cloned.1.call-start
  35.6 0.0 copy-done.2
  35.7 0.6 fusion.30
  36.2 1.1 iota_compare_fusion
  37.4 1.3 iota_compare_fusion.2
  38.7 42.7 %all-gather.5.cloned.1.call-done = bf16[4,256,1024]{1,2,0:T(8,128)(2,1)} async-done(((bf16[4,256,256]{1,2,0:T(8,128)(2,1)}), bf16[4,256,1024]{1,2,0:T(8,128)(2,1)}) %all-gather.5.cloned.1.call-update) | async-done | bytes 2097168 | tf_op jit(solution)/shard_map/all_gather | solution.py:32
  81.4 0.0 copy-done
  81.4 2.4 %fusion.32 = f32[4,256,256]{2,1,0:T(8,128)S(1)} fusion(bf16[4,256,1024]{1,2,0:T(8,128)(2,1)} %all-gather.5.cloned.1.call-done, bf16[4,256,1024]{2,1,0:T(8,128)(2,1)S(1)} %copy-done), kind=kOutput, calls=%fused_computation.56 | convolution fusion | flops 536870912 | bytes 5242880 | tf_op jit(solution)/shard_map/txl,tml->txm/dot_general | solution.py:30
  83.9 0.0 copy-start.1
  83.9 0.0 copy-start.3
  83.9 0.1 slice_bitcast_fusion.3
  84.0 1.0 select_add_fusion
  85.0 0.0 all-reduce.3.cloned.1.call-update
  85.0 27.6 %all-reduce.3.cloned.1.call-done = f32[2,256,256]{2,1,0:T(8,128)} async-done(((f32[2,256,256]{2,1,0:T(8,128)}), f32[2,256,256]{2,1,0:T(8,128)}) %all-reduce.3.cloned.1.call-update) | async-done | bytes 524304 | tf_op jit(solution)/shard_map/psum | solution.py:40
  112.6 0.0 copy-done.1
  112.6 0.0 copy-done.3
  112.6 2.0 %fusion.6 = (f32[]{:T(128)}, f32[]{:T(128)}) fusion(f32[2,256,256]{2,1,0:T(8,128)} %all-reduce.3.cloned.1.call-done, f32[2]{0:T(128)S(1)} %copy-done.3, pred[2,256]{1,0:T(4,128)(4,1)S(1)} %get-tuple-element.20, pred[2,256]{1,0:T(4,128)(4,1)S(1)} %get-tuple-element.21, bf16[2,256,256]{2,1,0:T(8,128)(2,1)S(1)} %copy-done.1), kind=kLoop, calls=%fused_computation.16 | loop fusion | flops 1310718 | bytes 787472 | tf_op jit(solution)/shard_map/reduce_sum | solution.py:43
  114.6 33.8 %all-reduce = (f32[]{:T(128)}, f32[]{:T(128)}) all-reduce(f32[]{:T(128)} %get-tuple-element.3, f32[]{:T(128)} %get-tuple-element.2), channel_id=1, replica_groups=mesh['terms'=2,'rows'=4,'cols'=4] {'rows','cols'}, use_global_device_ids=true, to_apply=%region_2.3 | all-reduce | flops 2 | bytes 16 | tf_op jit(solution)/shard_map/psum | solution.py:42
  149.6 2.1 %fusion.8 = (bf16[2,256,256]{2,1,0:T(8,128)(2,1)}, bf16[2,256,256]{2,1,0:T(8,128)(2,1)}) fusion(f32[]{:T(128)S(6)} %div.3, f32[2,256,256]{2,1,0:T(8,128)} %all-reduce.3.cloned.1.call-done, f32[2]{0:T(128)S(1)} %copy-done.3, pred[2,256]{1,0:T(4,128)(4,1)S(1)} %get-tuple-element.20, pred[2,256]{1,0:T(4,128)(4,1)S(1)} %get-tuple-element.21, ...), kind=kLoop, calls=%fused_computation.18 | loop fusion | flops 1310720 | bytes 1311756 | tf_op jit(solution)/shard_map/convert_element_type | solution.py:47
  (2 shorter events, 0.0 us)
Async XLA Ops:
  7.2 74.2 %copy-start = (bf16[4,256,1024]{2,1,0:T(8,128)(2,1)S(1)}, bf16[4,256,1024]{2,1,0:T(8,128)(2,1)}, u32[]{:S(2)}) copy-start(bf16[4,256,1024]{2,1,0:T(8,128)(2,1)} %param.13) | copy-start | bytes 6291460
  7.2 22.4 %all-gather.3.cloned.1.call-start = ((), (), s32[]{:S(2)}) async-start(), calls=%async_computation | async-start | bytes 1310720 | tf_op jit(solution)/shard_map/all_gather | solution.py:20
  10.0 71.4 %all-gather.5.cloned.1.call-start = ((), (), s32[]{:S(2)}) async-start(), calls=%async_computation.1 | async-start | bytes 2621440 | tf_op jit(solution)/shard_map/all_gather | solution.py:32
  29.6 3.3 %copy-start.4 = (bf16[4,256,1024]{2,1,0:T(8,128)(2,1)S(1)}, bf16[4,256,1024]{2,1,0:T(8,128)(2,1)}, u32[]{:S(2)}) copy-start(bf16[4,256,1024]{2,1,0:T(8,128)(2,1)} %param.12) | copy-start | bytes 6291460
  29.6 4.7 %copy-start.5 = (bf16[2,1024,256]{2,1,0:T(8,128)(2,1)S(1)}, bf16[2,1024,256]{2,1,0:T(8,128)(2,1)}, u32[]{:S(2)}) copy-start(bf16[2,1024,256]{2,1,0:T(8,128)(2,1)} %all-gather.3.cloned.1.call-done) | copy-start | bytes 3145732
  32.9 2.7 %copy-start.2 = (s32[4]{0:T(128)S(1)}, s32[4]{0:T(128)}, u32[]{:S(2)}) copy-start(s32[4]{0:T(128)} %param.15) | copy-start | bytes 52
  35.6 77.0 %all-reduce.3.cloned.1.call-start = ((), (), s32[]{:S(2)}) async-start(), calls=%async_computation.2 | async-start | bytes 1048576 | tf_op jit(solution)/shard_map/psum | solution.py:40
  83.9 28.7 %copy-start.1 = (bf16[2,256,256]{2,1,0:T(8,128)(2,1)S(1)}, bf16[2,256,256]{2,1,0:T(8,128)(2,1)}, u32[]{:S(2)}) copy-start(bf16[2,256,256]{2,1,0:T(8,128)(2,1)} %param.8) | copy-start | bytes 786436
  83.9 28.7 %copy-start.3 = (f32[2]{0:T(128)S(1)}, f32[2]{0:T(128)}, u32[]{:S(2)}) copy-start(f32[2]{0:T(128)} %param.9) | copy-start | bytes 28
Sparse Core Ops, SparseCore 0:
  10.1 19.4 all-gather.2
  35.7 45.6 all-gather.4
  85.1 27.4 all-reduce.2
where the time goes:
time: 159 us; the launch traced here: 158 us
  waiting for transfers between devices  80.8 us (51%)
  blocking collectives  33.8 us (21%)
  between operations  23 us (14%)
  other arithmetic  11 us (7%)
  matrix products  7.45 us (5%)
  local copies, waits for them, and re-layouts  2.17 us (1%)
    all_gather x1, waiting for transfers between devices, per_device(): lax.all_gather(products, 'cols', axis=2, tiled=True)  42.7 us
    psum x1, blocking collectives, per_device(): lax.psum((jnp.sum(live_f * full_sigma), jnp.sum(live_f * live_f)), ('rows...  33.8 us
    psum x1, waiting for transfers between devices, per_device(): summed = lax.psum(partial_value, 'terms')  27.6 us
    all_gather x1, waiting for transfers between devices, per_device(): panels = lax.all_gather(live_psi, 'rows', axis=1, tiled=True)  10.4 us
    dot_general x4, matrix products, per_device(): jnp.dot(left_ops[term_index], col_panel, preferred_element_type=jnp.float32)  5 us
  transfers between devices with their start and end apart: 3, of which 3 were waited for; matrix products, arithmetic and copies ran while one was open for 3% of the time, Pallas kernels for 0%

commit v1 on v0

--- a/solution.py
+++ b/solution.py
@@ -37,7 +37,7 @@
         hit = (sector_ids == target[term_index])[:, None, None]
         partial_value = partial_value + jnp.where(hit, additions[term_index][None], 0.0)
     live_f = live_psi.astype(jnp.float32)
-    summed = lax.psum(partial_value, "terms")
+    summed = jnp.sum(lax.all_gather(partial_value, "terms"), axis=0)
     full_sigma = jnp.where(inside, summed + energy[:, None, None] * live_f, 0.0)
     numerator, denominator = lax.psum(
         (jnp.sum(live_f * full_sigma), jnp.sum(live_f * live_f)), ("rows", "cols")

time: 159 us -> 151 us (0.950)
  waiting for transfers between devices: 80.8 us -> 73.4 us
    psum x1 -> x0, waiting for transfers between devices: 27.6 us -> none  [per_device(): summed = lax.psum(partial_value, 'terms')]
    all_gather x0 -> x1, waiting for transfers between devices: none -> 20.2 us  [per_device(): summed = jnp.sum(lax.all_gather(partial_value, 'terms'), axis=0)]
where the time goes in v1:
time: 151 us; the launch traced here: 150 us
  waiting for transfers between devices  73.4 us (49%)
  blocking collectives  33.8 us (22%)
  between operations  23 us (15%)
  other arithmetic  10.3 us (7%)
  matrix products  7.45 us (5%)
  local copies, waits for them, and re-layouts  2.17 us (1%)
    all_gather x1, waiting for transfers between devices, per_device(): lax.all_gather(products, 'cols', axis=2, tiled=True)  42.7 us
    psum x1, blocking collectives, per_device(): lax.psum((jnp.sum(live_f * full_sigma), jnp.sum(live_f * live_f)), ('rows...  33.8 us
    all_gather x1, waiting for transfers between devices, per_device(): summed = jnp.sum(lax.all_gather(partial_value, 'terms'), axis=0)  20.2 us
    all_gather x1, waiting for transfers between devices, per_device(): panels = lax.all_gather(live_psi, 'rows', axis=1, tiled=True)  10.4 us
    dot_general x4, matrix products, per_device(): jnp.dot(left_ops[term_index], col_panel, preferred_element_type=jnp.float32)  5 us
  transfers between devices with their start and end apart: 3, of which 3 were waited for; matrix products, arithmetic and copies ran while one was open for 3% of the time, Pallas kernels for 0%

profile of v1, /device:TPU:0, one launch (start us, length us, event | category | flops | bytes accessed | tf_op | source)
XLA Modules:
  0.0 150.2 jit_solution(420277517362419652)
XLA Ops:
  7.2 0.0 copy-start
  7.2 0.0 all-gather.4.cloned.1.call-start
  7.3 0.9 broadcast_compare_fusion
  8.1 1.8 %and_select_fusion.1 = bf16[2,256,256]{2,1,0:T(8,128)(2,1)} fusion(bf16[2,256,256]{2,1,0:T(8,128)(2,1)} %param.8, pred[2,256]{1,0:T(4,128)(4,1)S(1)} %get-tuple-element.20, pred[2,256]{1,0:T(4,128)(4,1)S(1)} %get-tuple-element.21), kind=kLoop, calls=%fused_computation.13 | loop fusion | flops 262144 | bytes 525312 | tf_op jit(solution)/shard_map/jit(_where)/select_n | solution.py:17
  9.9 0.0 all-gather.4.cloned.1.call-update
  10.0 0.0 all-gather.6.cloned.1.call-start
  10.0 1.5 fusion.31
  19.3 10.4 %all-gather.4.cloned.1.call-done = bf16[2,1024,256]{2,1,0:T(8,128)(2,1)} async-done(((bf16[2,256,256]{2,1,0:T(8,128)(2,1)}), bf16[2,1024,256]{2,1,0:T(8,128)(2,1)}) %all-gather.4.cloned.1.call-update) | async-done | bytes 1048592 | tf_op jit(solution)/shard_map/all_gather | solution.py:20
  29.6 0.0 copy-start.4
  29.6 0.0 copy-start.5
  29.6 1.7 %fusion = bf16[1,256,256]{1,2,0:T(8,128)(2,1)S(1)} fusion(bf16[4,256,1024]{2,1,0:T(8,128)(2,1)} %param.12, bf16[2,1024,256]{2,1,0:T(8,128)(2,1)} %all-gather.4.cloned.1.call-done, s32[]{:T(128)S(6)} %select_n.63), kind=kOutput, calls=%fused_computation.4 | convolution fusion | flops 134283264 | bytes 1179652 | tf_op jit(solution)/shard_map/dot_general | solution.py:25
  31.3 1.6 %fusion.1 = bf16[1,256,256]{1,2,0:T(8,128)(2,1)S(1)} fusion(bf16[4,256,1024]{2,1,0:T(8,128)(2,1)} %param.12, bf16[2,1024,256]{2,1,0:T(8,128)(2,1)} %all-gather.4.cloned.1.call-done, s32[]{:T(128)S(6)} %select_n.64), kind=kOutput, calls=%fused_computation.5 | convolution fusion | flops 134283264 | bytes 1179652 | tf_op jit(solution)/shard_map/dot_general | solution.py:25
  32.9 0.0 copy-done.4
  32.9 0.0 copy-start.2
  32.9 1.4 fusion.2
  34.3 0.0 copy-done.5
  34.3 0.4 fusion.3
  34.7 0.9 pad_maximum_fusion
  35.6 0.0 all-gather.6.cloned.1.call-update
  35.6 0.0 all-gather.8.cloned.1.call-start
  35.6 0.0 copy-done.2
  35.7 0.6 fusion.30
  36.2 1.1 iota_compare_fusion
  37.4 1.3 iota_compare_fusion.2
  38.7 42.7 %all-gather.6.cloned.1.call-done = bf16[4,256,1024]{1,2,0:T(8,128)(2,1)} async-done(((bf16[4,256,256]{1,2,0:T(8,128)(2,1)}), bf16[4,256,1024]{1,2,0:T(8,128)(2,1)}) %all-gather.6.cloned.1.call-update) | async-done | bytes 2097168 | tf_op jit(solution)/shard_map/all_gather | solution.py:32
  81.4 0.0 copy-done
  81.4 2.4 %fusion.32 = f32[4,256,256]{2,1,0:T(8,128)S(1)} fusion(bf16[4,256,1024]{1,2,0:T(8,128)(2,1)} %all-gather.6.cloned.1.call-done, bf16[4,256,1024]{2,1,0:T(8,128)(2,1)S(1)} %copy-done), kind=kOutput, calls=%fused_computation.56 | convolution fusion | flops 536870912 | bytes 5242880 | tf_op jit(solution)/shard_map/txl,tml->txm/dot_general | solution.py:30
  83.9 0.1 slice_bitcast_fusion.3
  83.9 0.0 copy-start.1
  84.0 0.0 copy-start.3
  84.0 1.0 select_add_fusion
  85.0 0.0 all-gather.8.cloned.1.call-update
  85.0 20.2 %all-gather.8.cloned.1.call-done = f32[2,2,256,256]{3,2,1,0:T(8,128)} async-done(((f32[1,2,256,256]{3,2,1,0:T(8,128)}), f32[2,2,256,256]{3,2,1,0:T(8,128)}) %all-gather.8.cloned.1.call-update) | async-done | bytes 1048592 | tf_op jit(solution)/shard_map/all_gather | solution.py:40
  105.2 1.4 reduce_sum.27
  106.6 0.0 copy-done.1
  106.6 0.0 copy-done.3
  106.6 0.9 fusion.6
  107.6 33.8 %all-reduce = (f32[]{:T(128)}, f32[]{:T(128)}) all-reduce(f32[]{:T(128)} %get-tuple-element.3, f32[]{:T(128)} %get-tuple-element.2), channel_id=1, replica_groups=mesh['terms'=2,'rows'=4,'cols'=4] {'rows','cols'}, use_global_device_ids=true, to_apply=%region_2.3 | all-reduce | flops 2 | bytes 16 | tf_op jit(solution)/shard_map/psum | solution.py:42
  142.6 1.0 fusion.8
  (2 shorter events, 0.0 us)
Async XLA Ops:
  7.2 74.2 %copy-start = (bf16[4,256,1024]{2,1,0:T(8,128)(2,1)S(1)}, bf16[4,256,1024]{2,1,0:T(8,128)(2,1)}, u32[]{:S(2)}) copy-start(bf16[4,256,1024]{2,1,0:T(8,128)(2,1)} %param.13) | copy-start | bytes 6291460
  7.2 22.4 %all-gather.4.cloned.1.call-start = ((), (), s32[]{:S(2)}) async-start(), calls=%async_computation | async-start | bytes 1310720 | tf_op jit(solution)/shard_map/all_gather | solution.py:20
  10.0 71.4 %all-gather.6.cloned.1.call-start = ((), (), s32[]{:S(2)}) async-start(), calls=%async_computation.1 | async-start | bytes 2621440 | tf_op jit(solution)/shard_map/all_gather | solution.py:32
  29.6 3.3 %copy-start.4 = (bf16[4,256,1024]{2,1,0:T(8,128)(2,1)S(1)}, bf16[4,256,1024]{2,1,0:T(8,128)(2,1)}, u32[]{:S(2)}) copy-start(bf16[4,256,1024]{2,1,0:T(8,128)(2,1)} %param.12) | copy-start | bytes 6291460
  29.6 4.7 %copy-start.5 = (bf16[2,1024,256]{2,1,0:T(8,128)(2,1)S(1)}, bf16[2,1024,256]{2,1,0:T(8,128)(2,1)}, u32[]{:S(2)}) copy-start(bf16[2,1024,256]{2,1,0:T(8,128)(2,1)} %all-gather.4.cloned.1.call-done) | copy-start | bytes 3145732
  32.9 2.7 %copy-start.2 = (s32[4]{0:T(128)S(1)}, s32[4]{0:T(128)}, u32[]{:S(2)}) copy-start(s32[4]{0:T(128)} %param.15) | copy-start | bytes 52
  35.6 69.6 %all-gather.8.cloned.1.call-start = ((), (), s32[]{:S(2)}) async-start(), calls=%async_computation.2 | async-start | bytes 1572864 | tf_op jit(solution)/shard_map/all_gather | solution.py:40
  83.9 22.7 %copy-start.1 = (bf16[2,256,256]{2,1,0:T(8,128)(2,1)S(1)}, bf16[2,256,256]{2,1,0:T(8,128)(2,1)}, u32[]{:S(2)}) copy-start(bf16[2,256,256]{2,1,0:T(8,128)(2,1)} %param.8) | copy-start | bytes 786436
  84.0 22.7 %copy-start.3 = (f32[2]{0:T(128)S(1)}, f32[2]{0:T(128)}, u32[]{:S(2)}) copy-start(f32[2]{0:T(128)} %param.9) | copy-start | bytes 28
Sparse Core Ops, SparseCore 0:
  10.1 19.4 all-gather.3
  35.7 45.6 all-gather.5
  85.1 20.0 all-gather.7
